TPU v7x, 32 devices: a whole 2x2x4 slice. The times are simulated.
32 devices in a mesh: lat: 16 (over z, x, core), tm: 2 (over y).
Axes of the slice: x: 2, y: 2, z: 4, core: 2. Of those that a mesh axis runs over, the one named last changes fastest.
Arguments:
- fields: bfloat16 [512, 64, 1024], P('lat', 'tm'), may hold values from -16 to 16
Outputs:
- covariance: float32 [64, 64], P('tm')
All inputs are finite; a program needn't handle non-finite values.
Results may differ from a plain program's by a relative error of at most 0.0003.
Values may be sent and summed in bfloat16 or wider, within the bound.
A program may use at most 64 MiB of HBM per device.

v0:
```python
import math
import jax
import jax.numpy as jnp
from jax import lax
from jax.sharding import PartitionSpec as P

TRUNC = 341
MSLOT = 384
DSLOT = 384


def start_value(order, sine_lat):
    log_start = 0.5 * (
        math.log(0.5)
        + lax.lgamma(order + 1.5)
        - (0.5 * math.log(math.pi) - math.log(2.0))
        - lax.lgamma(order + 1.0)
    ) + order * jnp.log(sine_lat)
    taper = jnp.clip((log_start + 70.0) / 10.0, 0.0, 1.0)
    return jnp.exp(jnp.maximum(log_start, -80.0)) * taper


def step_factors(order, degree):
    top = jnp.sqrt((4.0 * degree * degree - 1.0) / (degree * degree - order * order))
    below = degree - 1.0
    back = jnp.sqrt(
        jnp.maximum(below * below - order * order, 0.0) / jnp.abs(4.0 * below * below - 1.0)
    )
    return (top, top * back)


def legendre_blocks(orders, cosine_lat, sine_lat):
    order_total = orders.shape[0]
    lat_total = cosine_lat.shape[0]
    block_total = 16
    block_length = DSLOT // block_total
    order_grid = orders[:, None, None]
    cosine_grid = cosine_lat[None, :, None]
    block_base = (jnp.arange(block_total) * block_length).astype(jnp.float32)[None, None, :]
    unit = jnp.ones((order_total, lat_total, block_total), jnp.float32)
    empty = jnp.zeros_like(unit)

    def compose(position, matrices):
        upper_left, upper_right, lower_left, lower_right = matrices
        top, mixed = step_factors(
            order_grid, order_grid + block_base + position.astype(jnp.float32)
        )
        diagonal_term = top * cosine_grid
        return (
            diagonal_term * upper_left - mixed * lower_left,
            diagonal_term * upper_right - mixed * lower_right,
            upper_left,
            upper_right,
        )

    upper_left, upper_right, lower_left, lower_right = lax.fori_loop(
        1, block_length + 1, compose, (unit, empty, empty, unit)
    )
    current = start_value(orders[:, None], sine_lat[None, :])
    previous = jnp.zeros_like(current)
    current_list = []
    previous_list = []
    for block in range(block_total):
        current_list.append(current)
        previous_list.append(previous)
        current, previous = (
            upper_left[:, :, block] * current + upper_right[:, :, block] * previous,
            lower_left[:, :, block] * current + lower_right[:, :, block] * previous,
        )
    current = jnp.stack(current_list, axis=-1)
    previous = jnp.stack(previous_list, axis=-1)
    outputs = []
    for position in range(1, block_length + 1):
        outputs.append(current)
        top, mixed = step_factors(order_grid, order_grid + block_base + float(position))
        current, previous = (top * cosine_grid * current - mixed * previous, current)
    values = jnp.stack(outputs, axis=-1)
    return values.reshape(order_total, lat_total, DSLOT)


def weighted_basis(orders, cosine_lat, sine_lat, weight):
    values = legendre_blocks(orders, cosine_lat, sine_lat)
    offsets = jnp.arange(DSLOT).astype(jnp.float32)
    keep = (orders[:, None] + offsets[None, :] <= TRUNC).astype(jnp.float32)
    factor = jnp.where(orders > 0, math.sqrt(2.0), 1.0)
    table = values * keep[:, None, :] * weight[None, :, None] * factor[:, None, None]
    return table.astype(jnp.bfloat16)


def local(fields):
    row_count, month_count, lon_count = fields.shape
    lat_devices = lax.axis_size("lat")
    slots_dev = MSLOT // lat_devices
    lat_index = lax.axis_index("lat")
    column = jnp.arange(2 * MSLOT)
    group = column // (2 * slots_dev)
    inner = column % (2 * slots_dev) // 2
    part_index = column % 2
    own_inner = jnp.arange(slots_dev)
    wave_order = group * slots_dev + inner
    own_order = lat_index * slots_dev + own_inner
    longitude = jnp.arange(lon_count)
    phase = (
        2.0
        * math.pi
        * (wave_order[:, None] * longitude[None, :] % lon_count).astype(jnp.float32)
        / lon_count
    )
    active = (wave_order <= TRUNC).astype(jnp.float32)[:, None]
    transform = (
        jnp.where(part_index[:, None] == 0, jnp.cos(phase), -jnp.sin(phase))
        * active
        / math.sqrt(lon_count)
    )
    transform = transform.astype(jnp.bfloat16)
    flat_fields = fields.reshape(row_count * month_count, lon_count)
    fourier = lax.dot_general(
        transform, flat_fields, (((1,), (1,)), ((), ())), preferred_element_type=jnp.float32
    )
    fourier = fourier.astype(jnp.bfloat16).reshape(2 * MSLOT, row_count, month_count)
    moved = lax.all_to_all(fourier, "lat", split_axis=0, concat_axis=1, tiled=True)
    lat_count = moved.shape[1]
    theta = math.pi * (jnp.arange(lat_count).astype(jnp.float32) + 0.5) / lat_count
    cosine_lat = jnp.cos(theta)
    sine_lat = jnp.sin(theta)
    weight = math.pi * sine_lat / lat_count
    basis = weighted_basis(own_order.astype(jnp.float32), cosine_lat, sine_lat, weight)
    moved_data = moved.reshape(slots_dev, 2, lat_count, month_count)
    coefficients = jnp.einsum(
        "srjt,sjd->tsrd", moved_data, basis, preferred_element_type=jnp.float32
    )
    coefficients = coefficients.astype(jnp.bfloat16).reshape(month_count, -1)
    tm_devices = lax.axis_size("tm")
    total_months = month_count * tm_devices
    columns = lax.all_to_all(coefficients, "tm", split_axis=1, concat_axis=0, tiled=True)
    partial_gram = lax.psum_scatter(
        lax.dot_general(
            columns, columns, (((1,), (1,)), ((), ())), preferred_element_type=jnp.float32
        ),
        "tm",
        scatter_dimension=0,
        tiled=True,
    )
    gram = lax.psum(partial_gram, "lat")
    own_block = lax.dynamic_slice_in_dim(gram, lax.axis_index("tm") * month_count, month_count, 1)
    trace_total = lax.psum(jnp.sum(jnp.diagonal(own_block)), "tm")
    return total_months * gram / (trace_total + 1e-06)


def solution(mesh):
    placed = (P("lat", "tm", None),)
    return jax.shard_map(
        local, mesh=mesh, in_specs=placed, out_specs=P("tm", None), check_vma=False
    )
```

profile of v0, /device:TPU:0, one launch (start us, length us, event | category | flops | bytes accessed | tf_op | source)
XLA Modules:
  0.0 353.8 jit_solution(13318265986543368269)
XLA Ops:
  8.1 16.4 %convolution_convert_fusion = bf16[768,1024]{1,0:T(8,128)(2,1)} fusion(bf16[1024,1024]{1,0:T(8,128)(2,1)S(1)} %bitcast.84, f32[768]{0:T(1024)S(1)} %get-tuple-element.432, s32[768]{0:T(1024)S(1)} %fusion.324, pred[768]{0:T(1024)(128)(4,1)S(1)} %get-tuple-element.431), kind=kOutput, calls=%fused_computation.41 | convolution fusion | flops 1626341376 | bytes 3676928 | tf_op jit(solution)/shard_map/dot_general | solution.py:117
  26.2 9.2 %copy.128 = bf16[768,32,32]{2,1,0:T(8,128)(2,1)} copy(bf16[768,32,32]{0,2,1:T(8,128)(2,1)S(1)} %bitcast.90) | data formatting | bytes 3145728 | tf_op jit(solution)/shard_map/reshape | solution.py:120
  35.4 9.3 %reshape.8823 = bf16[16,2,24576]{2,1,0:T(2,128)(2,1)} reshape(bf16[768,32,32]{2,1,0:T(8,128)(2,1)} %copy.128) | data formatting | bytes 3145728
  44.7 7.4 %all-to-all-start = ((bf16[16,2,24576]{2,1,0:T(2,128)(2,1)}), bf16[16,2,24576]{2,1,0:T(2,128)(2,1)}, u32[]{:S(2)}, u32[]{:S(2)}) async-start(bf16[16,2,24576]{2,1,0:T(2,128)(2,1)} %reshape.8823), calls=%async_computation | async-start | bytes 3145728 | tf_op jit(solution)/shard_map/all_to_all | solution.py:121
  53.3 71.6 %while.25 = (s32[]{:T(128)}, f32[24,512,16]{1,2,0:T(8,128)S(1)}, f32[24,512,16]{1,2,0:T(8,128)}, f32[24,512,16]{1,2,0:T(8,128)S(1)}, f32[24,512,16]{1,2,0:T(8,128)S(1)}, /*index=5*/s32[]{:T(128)}, s32[]{:T(128)}, s32[]{:T(128)}) while((s32[]{:T(128)}, f32[24,512,16]{1,2,0:T(8,128)S(1)}, ...), condition=%wide.region_1.2_spmd.clone.clone.clone, body=%wide.region_0.1_spmd.clone.clone.clone.sunk | while | flops 1778076 | bytes 6308475 | solution.py:56
  58.6 2.7 fusion.362
  61.6 2.7 fusion.362
  64.6 2.7 fusion.362
  67.6 2.7 fusion.362
  70.7 2.7 fusion.362
  73.7 2.7 fusion.362
  79.8 2.7 fusion.362
  125.6 6.1 %add_bitcast_fusion = (f32[24,512,1,1]{1,2,3,0:T(1,128)S(1)}, f32[24,512,1]{1,2,0:T(1,128)S(1)}, f32[24,512,1]{1,2,0:T(1,128)S(1)}, f32[24,512,1]{1,2,0:T(1,128)...) fusion(f32[24,512,16]{1,2,0:T(8,128)S(1)} %get-tuple-element.24, ...), kind=kLoop, calls=%fused_computation.123 | loop fusion | flops 1155072 | bytes 4278464 | tf_op jit(solution)/shard_map/stack | solution.py:71
  152.9 3.0 stack.164
  186.8 17.4 %copy.126 = f32[24,512,16,24]{1,3,2,0:T(8,128)S(1)} copy(f32[24,512,16,24]{1,2,3,0:T(8,128)} %subtract_dynamic-update-slice_fusion) | data formatting | bytes 37748736 | tf_op jit(solution)/shard_map/stack | solution.py:77
  204.4 6.3 %fusion.20 = bf16[24,512,384]{1,2,0:T(8,128)(2,1)} fusion(f32[24,512,16,24]{1,3,2,0:T(8,128)S(1)} %copy.126, f32[24]{0:T(128)S(1)} %copy-done.23, f32[512]{0:T(512)S(1)} %fusion.337, f32[24,384]{1,0:T(8,128)S(1)} %fusion.38), kind=kLoop, calls=%fused_computation.30 | loop fusion | flops 18874368 | bytes 28350560 | tf_op jit(solution)/shard_map/convert_element_type | solution.py:87
  210.6 7.9 %reshape.8824 = bf16[768,32,32]{2,1,0:T(8,128)(2,1)} reshape(bf16[16,2,24576]{2,1,0:T(2,128)(2,1)} %all-to-all-done) | data formatting | bytes 3145728
  218.5 9.5 %copy.129 = bf16[16,48,32,32]{2,0,3,1:T(8,128)(2,1)} copy(bf16[16,48,32,32]{3,2,1,0:T(8,128)(2,1)} %bitcast.85) | data formatting | bytes 3145728 | tf_op jit(solution)/shard_map/all_to_all | solution.py:121
  228.0 9.3 %reshape.8814 = bf16[24,2,512,32]{2,3,1,0:T(8,128)(2,1)} reshape(bf16[48,16,32,32]{2,1,3,0:T(8,128)(2,1)} %bitcast.86) | data formatting | bytes 3145728 | tf_op jit(solution)/shard_map/reshape | solution.py:128
  237.3 7.0 %fusion.352 = f32[24,384,64]{1,2,0:S(1)} fusion(bf16[24,512,384]{1,2,0:T(8,128)(2,1)} %fusion.20, bf16[24,512,64]{1,2,0:T(8,128)(2,1)} %bitcast.89), kind=kOutput, calls=%fused_computation.517 | convolution fusion | flops 603979776 | bytes 13369344
  248.6 18.3 %all_to_all.34 = bf16[32,2,9216]{2,0,1:T(8,128)(2,1)S(1)} all-to-all(bf16[32,2,9216]{2,0,1:T(8,128)(2,1)S(1)} %copy.132), channel_id=1, replica_groups=mesh['lat'=16,'tm'=2] {'tm'}, dimensions={1} | all-to-all | bytes 2359296 | tf_op jit(solution)/shard_map/all_to_all | solution.py:135
  267.9 10.2 %reduce-scatter.2.cloned.1.call-done = f32[32,64]{1,0:T(8,128)} async-done(((f32[64,64]{1,0:T(8,128)}), f32[32,64]{1,0:T(8,128)}) %reduce-scatter.2.cloned.1.call-update) | async-done | bytes 8208 | tf_op jit(solution)/shard_map/reduce_scatter | solution.py:136
  278.1 60.6 %psum.14 = f32[32,64]{1,0:T(8,128)S(1)} all-reduce(f32[32,64]{1,0:T(8,128)} %reduce-scatter.2.cloned.1.call-done), channel_id=1, replica_groups=mesh['lat'=16,'tm'=2] {'lat'}, use_global_device_ids=true, to_apply=%region_3.4 | all-reduce | flops 2048 | bytes 16384 | tf_op jit(solution)/shard_map/psum | solution.py:144
  340.1 5.5 %psum.15 = f32[]{:T(128)} all-reduce(f32[]{:T(128)} %reduce_sum.9), channel_id=1, replica_groups=mesh['lat'=16,'tm'=2] {'tm'}, use_global_device_ids=true, to_apply=%region_5.6 | all-reduce | flops 1 | bytes 8 | tf_op jit(solution)/shard_map/psum | solution.py:146
  (338 shorter events, 116.8 us)
Async XLA Ops:
  44.7 165.9 %all-to-all-start = ((bf16[16,2,24576]{2,1,0:T(2,128)(2,1)}), bf16[16,2,24576]{2,1,0:T(2,128)(2,1)}, u32[]{:S(2)}, u32[]{:S(2)}) async-start(bf16[16,2,24576]{2,1,0:T(2,128)(2,1)} %reshape.8823), calls=%async_computation | async-start | bytes 3145728 | tf_op jit(solution)/shard_map/all_to_all | solution.py:121
  52.2 226.0 %reduce-scatter.2.cloned.1.call-start = ((), (), s32[]{:S(2)}) async-start(), calls=%async_computation.3 | async-start | bytes 49152 | tf_op jit(solution)/shard_map/reduce_scatter | solution.py:136
  52.4 82.7 %copy-start.21 = (f32[24]{0:T(128)}, f32[24]{0:T(128)S(1)}, u32[]{:S(2)}) copy-start(f32[24]{0:T(128)S(1)} %add_convert_fusion) | copy-start | bytes 292
  152.8 13.9 %copy-start.13 = (f32[24,16]{1,0:T(8,128)S(1)}, f32[24,16]{1,0:T(8,128)}, u32[]{:S(2)}) copy-start(f32[24,16]{1,0:T(8,128)} %copy.93) | copy-start | bytes 4612
  152.8 17.5 %copy-start.12 = (f32[24,16]{1,0:T(8,128)S(1)}, f32[24,16]{1,0:T(8,128)}, u32[]{:S(2)}) copy-start(f32[24,16]{1,0:T(8,128)} %copy.100) | copy-start | bytes 4612
  152.8 17.5 %copy-start.14 = (f32[24,16]{1,0:T(8,128)S(1)}, f32[24,16]{1,0:T(8,128)}, u32[]{:S(2)}) copy-start(f32[24,16]{1,0:T(8,128)} %copy.99) | copy-start | bytes 4612
  152.8 18.8 %copy-start.9 = (f32[24,16]{1,0:T(8,128)S(1)}, f32[24,16]{1,0:T(8,128)}, u32[]{:S(2)}) copy-start(f32[24,16]{1,0:T(8,128)} %copy.101) | copy-start | bytes 4612
  152.8 18.8 %copy-start.11 = (f32[24,16]{1,0:T(8,128)S(1)}, f32[24,16]{1,0:T(8,128)}, u32[]{:S(2)}) copy-start(f32[24,16]{1,0:T(8,128)} %copy.102) | copy-start | bytes 4612
  157.1 18.2 %copy-start.8 = (f32[24,16]{1,0:T(8,128)S(1)}, f32[24,16]{1,0:T(8,128)}, u32[]{:S(2)}) copy-start(f32[24,16]{1,0:T(8,128)} %copy.107) | copy-start | bytes 4612
  157.1 18.2 %copy-start.10 = (f32[24,16]{1,0:T(8,128)S(1)}, f32[24,16]{1,0:T(8,128)}, u32[]{:S(2)}) copy-start(f32[24,16]{1,0:T(8,128)} %copy.108) | copy-start | bytes 4612
  158.3 18.3 %copy-start.6 = (f32[24,16]{1,0:T(8,128)S(1)}, f32[24,16]{1,0:T(8,128)}, u32[]{:S(2)}) copy-start(f32[24,16]{1,0:T(8,128)} %copy.109) | copy-start | bytes 4612
  158.3 18.3 %copy-start.7 = (f32[24,16]{1,0:T(8,128)S(1)}, f32[24,16]{1,0:T(8,128)}, u32[]{:S(2)}) copy-start(f32[24,16]{1,0:T(8,128)} %copy.110) | copy-start | bytes 4612
  162.3 16.7 %copy-start.4 = (f32[24,16]{1,0:T(8,128)S(1)}, f32[24,16]{1,0:T(8,128)}, u32[]{:S(2)}) copy-start(f32[24,16]{1,0:T(8,128)} %copy.113) | copy-start | bytes 4612
  162.3 16.7 %copy-start.5 = (f32[24,16]{1,0:T(8,128)S(1)}, f32[24,16]{1,0:T(8,128)}, u32[]{:S(2)}) copy-start(f32[24,16]{1,0:T(8,128)} %copy.114) | copy-start | bytes 4612
  164.6 15.6 %copy-start.2 = (f32[24,16]{1,0:T(8,128)S(1)}, f32[24,16]{1,0:T(8,128)}, u32[]{:S(2)}) copy-start(f32[24,16]{1,0:T(8,128)} %copy.115) | copy-start | bytes 4612
  164.6 15.7 %copy-start.3 = (f32[24,16]{1,0:T(8,128)S(1)}, f32[24,16]{1,0:T(8,128)}, u32[]{:S(2)}) copy-start(f32[24,16]{1,0:T(8,128)} %copy.116) | copy-start | bytes 4612
  168.0 14.5 %copy-start.20 = (f32[24,16]{0,1:T(8,128)S(1)}, f32[24,16]{0,1:T(8,128)}, u32[]{:S(2)}) copy-start(f32[24,16]{0,1:T(8,128)} %get-tuple-element.404) | copy-start | bytes 4612
  168.0 14.6 %copy-start.19 = (f32[24,16]{0,1:T(8,128)S(1)}, f32[24,16]{0,1:T(8,128)}, u32[]{:S(2)}) copy-start(f32[24,16]{0,1:T(8,128)} %get-tuple-element.408) | copy-start | bytes 4612
  168.0 14.7 %copy-start.18 = (f32[24,16]{0,1:T(8,128)S(1)}, f32[24,16]{0,1:T(8,128)}, u32[]{:S(2)}) copy-start(f32[24,16]{0,1:T(8,128)} %get-tuple-element.405) | copy-start | bytes 4612
  168.0 14.7 %copy-start.17 = (f32[24,16]{0,1:T(8,128)S(1)}, f32[24,16]{0,1:T(8,128)}, u32[]{:S(2)}) copy-start(f32[24,16]{0,1:T(8,128)} %get-tuple-element.407) | copy-start | bytes 4612
  168.0 14.8 %copy-start.16 = (f32[24,16]{0,1:T(8,128)S(1)}, f32[24,16]{0,1:T(8,128)}, u32[]{:S(2)}) copy-start(f32[24,16]{0,1:T(8,128)} %get-tuple-element.383) | copy-start | bytes 4612
  186.8 17.5 %copy-start.22 = (f32[24]{0:T(128)S(1)}, f32[24]{0:T(128)}, u32[]{:S(2)}) copy-start(f32[24]{0:T(128)} %copy-done.21) | copy-start | bytes 292
  186.8 17.5 %copy-start.23 = (f32[24]{0:T(128)S(1)}, f32[24]{0:T(128)}, u32[]{:S(2)}) copy-start(f32[24]{0:T(128)} %get-tuple-element.429) | copy-start | bytes 292
  218.5 128.4 %copy-start.1 = (bf16[32,32,1024]{2,1,0:T(8,128)(2,1)S(1)}, bf16[32,32,1024]{2,1,0:T(8,128)(2,1)}, u32[]{:S(2)}) copy-start(bf16[32,32,1024]{2,1,0:T(8,128)(2,1)} %param.3) | copy-start | bytes 6291460
  (2 other events, 15.5 us)
Sparse Core Ops, SparseCore 0:
  268.0 10.0 reduce-scatter.1
where the time goes:
time: 356 us; the launch traced here: 354 us
  other arithmetic  115 us (32%)
  local copies, waits for them, and re-layouts  96.8 us (27%)
  blocking collectives  84.4 us (24%)
  matrix products  24.4 us (7%)
  between operations  14.4 us (4%)
  waiting for transfers between devices  10.2 us (3%)
  starting transfers between devices  7.65 us (2%)
    sub x24, other arithmetic, compose(): diagonal_term * upper_right - mixed * lower_right  63.1 us
    psum x1, blocking collectives, local(): gram = lax.psum(partial_gram, 'lat')  60.6 us
    unnamed x24, other arithmetic  29 us
    unnamed x51, local copies, waits for them, and re-layouts  19.8 us
    all_to_all x1, blocking collectives, local(): lax.all_to_all(coefficients, 'tm', split_axis=1, concat_axis=0, tiled=True)  18.3 us
    another operation x1, local copies, waits for them, and re-layouts, legendre_blocks(): values = jnp.stack(outputs, axis=-1)  17.4 us
    dot_general x1, matrix products, local(): lax.dot_general(transform, flat_fields, (((1,), (1,)), ((), ())), preferr...  16.4 us
    reduce_scatter x1, waiting for transfers between devices, local(): lax.psum_scatter(lax.dot_general(columns, columns, (((1,), (1,)), ((), ()...  10.2 us
  transfers between devices with their start and end apart: 2, of which 1 were waited for; matrix products, arithmetic and copies ran while one was open for 45% of the time, Pallas kernels for 0%

commit v1 on v0

--- a/solution.py
+++ b/solution.py
@@ -141,7 +141,7 @@
         scatter_dimension=0,
         tiled=True,
     )
-    gram = lax.psum(partial_gram, "lat")
+    gram = lax.all_gather(partial_gram, "lat").sum(axis=0)
     own_block = lax.dynamic_slice_in_dim(gram, lax.axis_index("tm") * month_count, month_count, 1)
     trace_total = lax.psum(jnp.sum(jnp.diagonal(own_block)), "tm")
     return total_months * gram / (trace_total + 1e-06)

time: 356 us -> 280 us (0.79)
  other arithmetic: 115 us -> 66.3 us
  blocking collectives: 84.4 us -> 46.1 us
  local copies, waits for them, and re-layouts: 96.8 us -> 108 us
    psum x1 -> x0, blocking collectives: 60.6 us -> none  [local(): gram = lax.psum(partial_gram, 'lat')]
    sub x24, other arithmetic: 63.1 us -> 15.2 us  [compose(): diagonal_term * upper_right - mixed * lower_right]
    all_gather x0 -> x1, blocking collectives: none -> 22.3 us  [local(): gram = lax.all_gather(partial_gram, 'lat').sum(axis=0)]
    unnamed x51 -> x85, local copies, waits for them, and re-layouts: 19.8 us -> 20.4 us
  transfers between devices with their start and end apart: 2 -> 2, of which waited for: 1 -> 1; matrix products, arithmetic and copies ran while one was open for 45% -> 41% of each run, Pallas kernels for 0% -> 0%
where the time goes in v1:
time: 280 us; the launch traced here: 278 us
  local copies, waits for them, and re-layouts  108 us (39%)
  other arithmetic  66.3 us (24%)
  blocking collectives  46.1 us (16%)
  matrix products  24.5 us (9%)
  between operations  14.5 us (5%)
  waiting for transfers between devices  10.2 us (4%)
  starting transfers between devices  7.65 us (3%)
    unnamed x24, other arithmetic  30.4 us
    all_gather x1, blocking collectives, local(): gram = lax.all_gather(partial_gram, 'lat').sum(axis=0)  22.3 us
    unnamed x85, local copies, waits for them, and re-layouts  20.4 us
    all_to_all x1, blocking collectives, local(): lax.all_to_all(coefficients, 'tm', split_axis=1, concat_axis=0, tiled=True)  18.3 us
    another operation x1, local copies, waits for them, and re-layouts, legendre_blocks(): values = jnp.stack(outputs, axis=-1)  17.4 us
    dot_general x1, matrix products, local(): lax.dot_general(transform, flat_fields, (((1,), (1,)), ((), ())), preferr...  16.4 us
    sub x24, other arithmetic, compose(): diagonal_term * upper_right - mixed * lower_right  15.2 us
    mul x47, local copies, waits for them, and re-layouts, step_factors(): return (top, top * back)  12.3 us
  transfers between devices with their start and end apart: 2, of which 1 were waited for; matrix products, arithmetic and copies ran while one was open for 41% of the time, Pallas kernels for 0%

profile of v1, /device:TPU:0, one launch (start us, length us, event | category | flops | bytes accessed | tf_op | source)
XLA Modules:
  0.0 278.3 jit_solution(15512611404865712756)
XLA Ops:
  8.1 16.4 %convolution_convert_fusion = bf16[768,1024]{1,0:T(8,128)(2,1)} fusion(bf16[1024,1024]{1,0:T(8,128)(2,1)S(1)} %bitcast.85, f32[768]{0:T(1024)S(1)} %get-tuple-element.432, s32[768]{0:T(1024)S(1)} %fusion.324, pred[768]{0:T(1024)(128)(4,1)S(1)} %get-tuple-element.431), kind=kOutput, calls=%fused_computation.41 | convolution fusion | flops 1626341376 | bytes 3676928 | tf_op jit(solution)/shard_map/dot_general | solution.py:117
  26.2 9.2 %copy.128 = bf16[768,32,32]{2,1,0:T(8,128)(2,1)} copy(bf16[768,32,32]{0,2,1:T(8,128)(2,1)S(1)} %bitcast.91) | data formatting | bytes 3145728 | tf_op jit(solution)/shard_map/reshape | solution.py:120
  35.4 9.3 %reshape.8824 = bf16[16,2,24576]{2,1,0:T(2,128)(2,1)} reshape(bf16[768,32,32]{2,1,0:T(8,128)(2,1)} %copy.128) | data formatting | bytes 3145728
  44.8 7.4 %all-to-all-start = ((bf16[16,2,24576]{2,1,0:T(2,128)(2,1)}), bf16[16,2,24576]{2,1,0:T(2,128)(2,1)}, u32[]{:S(2)}, u32[]{:S(2)}) async-start(bf16[16,2,24576]{2,1,0:T(2,128)(2,1)} %reshape.8824), calls=%async_computation | async-start | bytes 3145728 | tf_op jit(solution)/shard_map/all_to_all | solution.py:121
  53.3 24.5 %while.25 = (s32[]{:T(128)}, f32[24,512,16]{1,2,0:T(8,128)S(1)}, f32[24,512,16]{1,2,0:T(8,128)S(1)}, f32[24,512,16]{1,2,0:T(8,128)S(1)}, f32[24,512,16]{1,2,0:T(8,128)S(1)}, /*index=5*/s32[]{:T(128)}, s32[]{:T(128)}, s32[]{:T(128)}) while((s32[]{:T(128)}, f32[24,512,16]{1,2,0:T(8,128)S(1)}, ...), condition=%wide.region_1.2_spmd.clone.clone.clone, body=%wide.region_0.1_spmd.clone.clone.clone.sunk | while | flops 1778076 | bytes 6308475 | solution.py:56
  78.7 4.1 %add_bitcast_fusion = (f32[24,512,1,1]{1,2,3,0:T(1,128)}, f32[24,512,1]{1,2,0:T(1,128)S(1)}, f32[24,512,1]{1,2,0:T(1,128)S(1)}, f32[24,512,1]{1,2,0:T(1,128)}, f...) fusion(f32[24,512,16]{1,2,0:T(8,128)S(1)} %get-tuple-element.24, ...), kind=kLoop, calls=%fused_computation.123 | loop fusion | flops 1155072 | bytes 4278464 | tf_op jit(solution)/shard_map/stack | solution.py:71
  83.4 2.1 stack.130
  107.5 2.1 stack.148
  109.8 3.2 %stack.164 = f32[24,512,16,1]{1,2,3,0:T(8,128)S(1)} concatenate(f32[24,512,1,1]{1,2,3,0:T(1,128)S(1)} %stack_broadcast_in_dim.3, f32[24,512,1,1]{1,2,3,0:T(1,128)} %bitcast.122, f32[24,512,1,1]{1,2,3,0:T(1,128)} %bitcast.121, f32[24,512,1,1]{1,2,3,0:T(1,128)} %bitcast.120, f32[24,512,1,1]{1,2,3,0:T(1,128)} %bitcast.119, f32[24,512,1,1]{1,2,3,0:T(1,128)} %bitcast.118, ...), dimensions={2} | concatenate | bytes 1572864 | tf_op jit(solution)/shard_map/stack | solution.py:71
  116.6 2.1 constant_dynamic-update-slice_fusion.15
  120.6 2.0 constant_dynamic-update-slice_fusion.13
  122.6 2.1 constant_dynamic-update-slice_fusion.12
  145.4 17.4 %copy.126 = f32[24,512,16,24]{1,3,2,0:T(8,128)S(1)} copy(f32[24,512,16,24]{1,2,3,0:T(8,128)} %subtract_dynamic-update-slice_fusion) | data formatting | bytes 37748736 | tf_op jit(solution)/shard_map/stack | solution.py:77
  162.9 6.6 %fusion.20 = bf16[24,512,384]{1,2,0:T(8,128)(2,1)} fusion(f32[24,512,16,24]{1,3,2,0:T(8,128)S(1)} %copy.126, f32[24]{0:T(128)S(1)} %copy-done.40, f32[512]{0:T(512)S(1)} %fusion.337, f32[24,384]{1,0:T(8,128)S(1)} %fusion.38), kind=kLoop, calls=%fused_computation.30 | loop fusion | flops 18874368 | bytes 28350560 | tf_op jit(solution)/shard_map/convert_element_type | solution.py:87
  169.5 7.9 %reshape.8825 = bf16[768,32,32]{2,1,0:T(8,128)(2,1)} reshape(bf16[16,2,24576]{2,1,0:T(2,128)(2,1)} %all-to-all-done) | data formatting | bytes 3145728
  177.4 9.4 %copy.129 = bf16[16,48,32,32]{2,0,3,1:T(8,128)(2,1)} copy(bf16[16,48,32,32]{3,2,1,0:T(8,128)(2,1)} %bitcast.86) | data formatting | bytes 3145728 | tf_op jit(solution)/shard_map/all_to_all | solution.py:121
  186.8 9.4 %reshape.8814 = bf16[24,2,512,32]{2,3,1,0:T(8,128)(2,1)} reshape(bf16[48,16,32,32]{2,1,3,0:T(8,128)(2,1)} %bitcast.87) | data formatting | bytes 3145728 | tf_op jit(solution)/shard_map/reshape | solution.py:128
  196.2 7.0 %fusion.352 = f32[24,384,64]{1,2,0:S(1)} fusion(bf16[24,512,384]{1,2,0:T(8,128)(2,1)} %fusion.20, bf16[24,512,64]{1,2,0:T(8,128)(2,1)} %bitcast.90), kind=kOutput, calls=%fused_computation.517 | convolution fusion | flops 603979776 | bytes 13369344
  203.5 2.0 copy.131
  205.4 4.5 %all_to_all.28 = bf16[32,2,9216]{2,1,0:T(2,128)(2,1)} reshape(bf16[32,24,2,384]{3,2,1,0:T(2,128)(2,1)} %copy.131) | data formatting | bytes 2359296 | tf_op jit(solution)/shard_map/all_to_all | solution.py:135
  211.4 18.3 %all_to_all.34 = bf16[32,2,9216]{2,0,1:T(8,128)(2,1)S(1)} all-to-all(bf16[32,2,9216]{2,0,1:T(8,128)(2,1)S(1)} %copy.132), channel_id=1, replica_groups=mesh['lat'=16,'tm'=2] {'tm'}, dimensions={1} | all-to-all | bytes 2359296 | tf_op jit(solution)/shard_map/all_to_all | solution.py:135
  230.8 10.2 %reduce-scatter.2.cloned.1.call-done = f32[32,64]{1,0:T(8,128)} async-done(((f32[64,64]{1,0:T(8,128)}), f32[32,64]{1,0:T(8,128)}) %reduce-scatter.2.cloned.1.call-update) | async-done | bytes 8208 | tf_op jit(solution)/shard_map/reduce_scatter | solution.py:136
  241.0 22.3 %all-gather = f32[512,64]{1,0:T(8,128)S(1)} all-gather(f32[32,64]{1,0:T(8,128)} %reduce-scatter.2.cloned.1.call-done), channel_id=2, replica_groups=mesh['lat'=16,'tm'=2] {'lat'}, dimensions={0}, use_global_device_ids=true | all-gather | bytes 139264 | tf_op jit(solution)/shard_map/all_gather | solution.py:144
  264.7 5.5 %psum.7 = f32[]{:T(128)} all-reduce(f32[]{:T(128)} %reduce_sum.19), channel_id=1, replica_groups=mesh['lat'=16,'tm'=2] {'tm'}, use_global_device_ids=true, to_apply=%region_5.6 | all-reduce | flops 1 | bytes 8 | tf_op jit(solution)/shard_map/psum | solution.py:146
  (373 shorter events, 82.1 us)
Async XLA Ops:
  44.8 124.8 %all-to-all-start = ((bf16[16,2,24576]{2,1,0:T(2,128)(2,1)}), bf16[16,2,24576]{2,1,0:T(2,128)(2,1)}, u32[]{:S(2)}, u32[]{:S(2)}) async-start(bf16[16,2,24576]{2,1,0:T(2,128)(2,1)} %reshape.8824), calls=%async_computation | async-start | bytes 3145728 | tf_op jit(solution)/shard_map/all_to_all | solution.py:121
  52.2 188.8 %reduce-scatter.2.cloned.1.call-start = ((), (), s32[]{:S(2)}) async-start(), calls=%async_computation.3 | async-start | bytes 49152 | tf_op jit(solution)/shard_map/reduce_scatter | solution.py:136
  52.5 34.0 %copy-start.38 = (f32[24]{0:T(128)}, f32[24]{0:T(128)S(1)}, u32[]{:S(2)}) copy-start(f32[24]{0:T(128)S(1)} %add_convert_fusion) | copy-start | bytes 292
  87.4 29.3 %copy-start.6 = (f32[24,16]{1,0:T(8,128)}, f32[24,16]{1,0:T(8,128)S(1)}, u32[]{:S(2)}) copy-start(f32[24,16]{1,0:T(8,128)S(1)} %copy.79) | copy-start | bytes 4612
  87.4 29.2 %copy-start.7 = (f32[24,16]{1,0:T(8,128)}, f32[24,16]{1,0:T(8,128)S(1)}, u32[]{:S(2)}) copy-start(f32[24,16]{1,0:T(8,128)S(1)} %copy.80) | copy-start | bytes 4612
  87.5 29.1 %copy-start.16 = (f32[24,16]{1,0:T(8,128)}, f32[24,16]{1,0:T(8,128)S(1)}, u32[]{:S(2)}) copy-start(f32[24,16]{1,0:T(8,128)S(1)} %copy.81) | copy-start | bytes 4612
  87.6 29.0 %copy-start.17 = (f32[24,16]{1,0:T(8,128)}, f32[24,16]{1,0:T(8,128)S(1)}, u32[]{:S(2)}) copy-start(f32[24,16]{1,0:T(8,128)S(1)} %copy.82) | copy-start | bytes 4612
  109.7 17.6 %copy-start.12 = (f32[24,16]{1,0:T(8,128)S(1)}, f32[24,16]{1,0:T(8,128)}, u32[]{:S(2)}) copy-start(f32[24,16]{1,0:T(8,128)} %copy.97) | copy-start | bytes 4612
  109.7 17.6 %copy-start.13 = (f32[24,16]{1,0:T(8,128)S(1)}, f32[24,16]{1,0:T(8,128)}, u32[]{:S(2)}) copy-start(f32[24,16]{1,0:T(8,128)} %copy.98) | copy-start | bytes 4612
  109.7 18.8 %copy-start.28 = (f32[24,16]{1,0:T(8,128)S(1)}, f32[24,16]{1,0:T(8,128)}, u32[]{:S(2)}) copy-start(f32[24,16]{1,0:T(8,128)} %copy.100) | copy-start | bytes 4612
  109.7 18.8 %copy-start.30 = (f32[24,16]{1,0:T(8,128)S(1)}, f32[24,16]{1,0:T(8,128)}, u32[]{:S(2)}) copy-start(f32[24,16]{1,0:T(8,128)} %copy.99) | copy-start | bytes 4612
  109.7 20.1 %copy-start.25 = (f32[24,16]{1,0:T(8,128)S(1)}, f32[24,16]{1,0:T(8,128)}, u32[]{:S(2)}) copy-start(f32[24,16]{1,0:T(8,128)} %copy.101) | copy-start | bytes 4612
  109.7 20.1 %copy-start.27 = (f32[24,16]{1,0:T(8,128)S(1)}, f32[24,16]{1,0:T(8,128)}, u32[]{:S(2)}) copy-start(f32[24,16]{1,0:T(8,128)} %copy.102) | copy-start | bytes 4612
  112.9 19.4 %copy-start.10 = (f32[24,16]{1,0:T(8,128)S(1)}, f32[24,16]{1,0:T(8,128)}, u32[]{:S(2)}) copy-start(f32[24,16]{1,0:T(8,128)} %copy.105) | copy-start | bytes 4612
  113.0 19.4 %copy-start.11 = (f32[24,16]{1,0:T(8,128)S(1)}, f32[24,16]{1,0:T(8,128)}, u32[]{:S(2)}) copy-start(f32[24,16]{1,0:T(8,128)} %copy.106) | copy-start | bytes 4612
  114.1 19.5 %copy-start.24 = (f32[24,16]{1,0:T(8,128)S(1)}, f32[24,16]{1,0:T(8,128)}, u32[]{:S(2)}) copy-start(f32[24,16]{1,0:T(8,128)} %copy.107) | copy-start | bytes 4612
  114.1 19.5 %copy-start.26 = (f32[24,16]{1,0:T(8,128)S(1)}, f32[24,16]{1,0:T(8,128)}, u32[]{:S(2)}) copy-start(f32[24,16]{1,0:T(8,128)} %copy.108) | copy-start | bytes 4612
  115.3 19.6 %copy-start.22 = (f32[24,16]{1,0:T(8,128)S(1)}, f32[24,16]{1,0:T(8,128)}, u32[]{:S(2)}) copy-start(f32[24,16]{1,0:T(8,128)} %copy.109) | copy-start | bytes 4612
  115.3 19.6 %copy-start.23 = (f32[24,16]{1,0:T(8,128)S(1)}, f32[24,16]{1,0:T(8,128)}, u32[]{:S(2)}) copy-start(f32[24,16]{1,0:T(8,128)} %copy.110) | copy-start | bytes 4612
  118.8 17.5 %copy-start.9 = (f32[24,16]{1,0:T(8,128)S(1)}, f32[24,16]{1,0:T(8,128)}, u32[]{:S(2)}) copy-start(f32[24,16]{1,0:T(8,128)} %copy.112) | copy-start | bytes 4612
  118.8 18.6 %copy-start.20 = (f32[24,16]{1,0:T(8,128)S(1)}, f32[24,16]{1,0:T(8,128)}, u32[]{:S(2)}) copy-start(f32[24,16]{1,0:T(8,128)} %copy.113) | copy-start | bytes 4612
  118.8 18.6 %copy-start.21 = (f32[24,16]{1,0:T(8,128)S(1)}, f32[24,16]{1,0:T(8,128)}, u32[]{:S(2)}) copy-start(f32[24,16]{1,0:T(8,128)} %copy.114) | copy-start | bytes 4612
  145.4 17.5 %copy-start.40 = (f32[24]{0:T(128)S(1)}, f32[24]{0:T(128)}, u32[]{:S(2)}) copy-start(f32[24]{0:T(128)} %get-tuple-element.429) | copy-start | bytes 292
  186.8 84.7 %copy-start.1 = (bf16[32,32,1024]{2,1,0:T(8,128)(2,1)S(1)}, bf16[32,32,1024]{2,1,0:T(8,128)(2,1)}, u32[]{:S(2)}) copy-start(bf16[32,32,1024]{2,1,0:T(8,128)(2,1)} %param.3) | copy-start | bytes 6291460
  (19 other events, 266.9 us)
Sparse Core Ops, SparseCore 0:
  230.9 10.0 reduce-scatter.1
